TPU v7x, 32 devices: a whole 2x2x4 slice. The times are simulated.
32 devices in a mesh: section: 4 (over y, x), tok: 8 (over z, core).
Axes of the slice: x: 2, y: 2, z: 4, core: 2. Of those that a mesh axis runs over, the one named last changes fastest.
Arguments:
- activations: bfloat16 [8, 2048, 8192], P('section', 'tok'), may hold values from -12 to 12
- projection: bfloat16 [8192, 512], P('tok'), may hold values from -0.0625 to 0.0625
Outputs:
- sketch: float32 [8, 512, 512], P('section', None, 'tok')
- similarity: float32 [8, 2], P('section')
All inputs are finite; a program needn't handle non-finite values.
Results may differ from a plain program's by a relative error of at most 0.0003.
Values may be sent and summed in bfloat16 or wider, within the bound.
A program may use at most 64 MiB of HBM per device.

v0:
```python
import jax
import jax.numpy as jnp
from jax import lax
from jax.sharding import PartitionSpec as P


def shifted(block, axis, distance):
    devices = range(lax.axis_size(axis))
    route = [(i - distance, i) for i in devices if i - distance in devices]
    return lax.ppermute(block, axis, route)


def frobenius(first, second):
    return jnp.sum(first * second, axis=(-2, -1))


def local_products(local_sketch, prev_last, next_first, section_index, sections):
    before = jnp.where(section_index == 0, local_sketch[0], prev_last)
    beyond = jnp.where(section_index == sections - 1, local_sketch[-1], next_first)
    squares = frobenius(local_sketch, local_sketch)
    chained = frobenius(local_sketch[:-1], local_sketch[1:])
    edges = jnp.stack(
        [
            frobenius(before, local_sketch[0]),
            frobenius(local_sketch[-1], beyond),
            frobenius(before, before),
            frobenius(beyond, beyond),
        ]
    )
    return jnp.concatenate([squares, chained, edges])


def finish(products, layers):
    squares = products[:layers]
    chained = products[layers : 2 * layers - 1]
    edges = products[2 * layers - 1 :]
    ext_squares = jnp.concatenate([edges[2:3], squares, edges[3:4]])
    ext_chained = jnp.concatenate([edges[0:1], chained, edges[1:2]])
    ratios = ext_chained / jnp.sqrt(ext_squares[:-1] * ext_squares[1:])
    return jnp.stack([ratios[:-1], ratios[1:]], axis=1)


def local(activations, projection):
    layers, tok_rows, model_width = activations.shape
    sketch_width = projection.shape[1]
    groups = lax.axis_size("tok")
    total_tokens = tok_rows * groups
    flat_acts = activations.reshape(layers * tok_rows, model_width)
    projected = jnp.dot(
        flat_acts,
        lax.all_gather(projection, "tok", axis=0, tiled=True),
        preferred_element_type=jnp.float32,
    )
    projected = projected.reshape(layers, tok_rows, sketch_width)
    raw_gram = jnp.einsum("ltr,lts->lrs", projected, projected, precision=lax.Precision.HIGHEST)
    local_sums = jnp.sum(projected, axis=1)
    tok_index = lax.axis_index("tok")
    section_index = lax.axis_index("section")
    sections = lax.axis_size("section")
    columns_dev = sketch_width // groups
    shares = lax.psum_scatter(raw_gram, "tok", scatter_dimension=2, tiled=True)
    totals = lax.psum(local_sums, "tok")
    local_totals = lax.dynamic_slice_in_dim(totals, tok_index * columns_dev, columns_dev, 1)
    local_sketch = shares - totals[:, :, None] * local_totals[:, None, :] / total_tokens
    next_first = shifted(local_sketch[0].astype(jnp.bfloat16), "section", -1).astype(jnp.float32)
    prev_last = shifted(local_sketch[layers - 1].astype(jnp.bfloat16), "section", 1).astype(
        jnp.float32
    )
    partial_products = local_products(local_sketch, prev_last, next_first, section_index, sections)
    products = lax.psum(partial_products, "tok")
    return (local_sketch, finish(products, layers))


def solution(mesh):
    return jax.shard_map(
        local,
        mesh=mesh,
        in_specs=(P("section", "tok", None), P("tok", None)),
        out_specs=(P("section", None, "tok"), P("section", None)),
        check_vma=False,
    )
```

profile of v0, /device:TPU:5, one launch (start us, length us, event | category | flops | bytes accessed | tf_op | source)
XLA Modules:
  0.0 181.1 jit_solution(8922740263490484385)
XLA Ops:
  7.2 0.0 all-gather.2.cloned.1.call-start
  7.2 0.7 all-gather.2.cloned.1.call-update
  7.9 0.0 reduce-scatter.2.cloned.1.call-start
  7.9 85.3 %all-gather.2.cloned.1.call-done = bf16[8192,512]{1,0:T(8,128)(2,1)} async-done(((bf16[1024,512]{1,0:T(8,128)(2,1)}), bf16[8192,512]{1,0:T(8,128)(2,1)}) %all-gather.2.cloned.1.call-update) | async-done | bytes 8388624 | tf_op jit(solution)/shard_map/all_gather | solution.py:51
  93.2 9.5 %fusion.6 = (f32[2,512]{1,0:T(2,128)S(1)}, f32[2,256,512]{2,1,0:T(8,128)S(1)}) fusion(bf16[2,256,8192]{2,1,0:T(8,128)(2,1)} %param.2, bf16[8192,512]{1,0:T(8,128)(2,1)} %all-gather.2.cloned.1.call-done), kind=kOutput, calls=%fused_computation.23 | convolution fusion | flops 4295228416 | bytes 17829888 | tf_op jit(solution)/shard_map/dot_general | solution.py:49
  102.7 3.3 %fusion.7 = f32[2,512,512]{1,2,0:T(8,128)} fusion(f32[2,256,512]{2,1,0:T(8,128)S(1)} %get-tuple-element.22), kind=kOutput, calls=%fused_computation.24 | convolution fusion | flops 1610612736 | bytes 3145728 | tf_op jit(solution)/shard_map/ltr,lts->lrs/dot_general | solution.py:55
  106.0 0.0 reduce-scatter.2.cloned.1.call-update
  106.1 13.5 %psum.14 = f32[2,512]{1,0:T(2,128)S(1)} all-reduce(f32[2,512]{1,0:T(2,128)S(1)} %get-tuple-element.21), channel_id=1, replica_groups=mesh['section'=4,'tok'=8] {'tok'}, use_global_device_ids=true, to_apply=%region_2.0 | all-reduce | flops 1024 | bytes 8192 | tf_op jit(solution)/shard_map/psum | solution.py:62
  119.6 0.1 constant_dynamic-slice_fusion
  119.7 18.1 %reduce-scatter.2.cloned.1.call-done = f32[2,512,64]{1,2,0:T(8,128)} async-done(((f32[2,512,512]{1,2,0:T(8,128)}), f32[2,512,64]{1,2,0:T(8,128)}) %reduce-scatter.2.cloned.1.call-update) | async-done | bytes 262160 | tf_op jit(solution)/shard_map/reduce_scatter | solution.py:61
  137.7 1.2 multiply_reduce_fusion
  138.9 0.0 copy-start
  138.9 3.1 %collective-permute-start.1 = (bf16[512,64]{0,1:T(8,128)(2,1)S(1)}, bf16[512,64]{0,1:T(8,128)(2,1)S(1)}, u32[]{:S(2)}, u32[]{:S(2)}) collective-permute-start(bf16[512,64]{0,1:T(8,128)(2,1)S(1)} %get-tuple-element.13), channel_id=1, source_target_pairs={{8,0},{16,8},{24,16},{9,1},{17,9},{25,17},{10,2},{18,10},{26,18},{... | collective-permute-start | bytes 196616 | tf_op jit(solution)/shard_map/ppermute | solution.py:10
  142.0 2.2 %collective-permute-start = (bf16[512,64]{0,1:T(8,128)(2,1)S(1)}, bf16[512,64]{0,1:T(8,128)(2,1)S(1)}, u32[]{:S(2)}, u32[]{:S(2)}) collective-permute-start(bf16[512,64]{0,1:T(8,128)(2,1)S(1)} %get-tuple-element.12), channel_id=1, source_target_pairs={{0,8},{8,16},{16,24},{1,9},{9,17},{17,25},{2,10},{10,18},{18,26},{... | collective-permute-start | bytes 196616 | tf_op jit(solution)/shard_map/ppermute | solution.py:10
  144.2 0.6 multiply_reduce_fusion.3
  144.8 0.0 collective-permute-done.1
  144.8 3.6 %collective-permute-done = bf16[512,64]{0,1:T(8,128)(2,1)S(1)} collective-permute-done((bf16[512,64]{0,1:T(8,128)(2,1)S(1)}, bf16[512,64]{0,1:T(8,128)(2,1)S(1)}, u32[]{:S(2)}, u32[]{:S(2)}) %collective-permute-start) | collective-permute-done | bytes 65568 | tf_op jit(solution)/shard_map/ppermute | solution.py:10
  148.4 0.7 multiply_reduce_fusion.1
  149.2 3.2 %concatenate.13 = f32[7]{0:T(128)S(1)} concatenate(f32[2]{0:T(128)S(1)} %get-tuple-element.10, f32[1]{0:T(128)} %bitcast.1, f32[1]{0:T(128)} %bitcast.4, f32[1]{0:T(128)} %bitcast.5, f32[1]{0:T(128)} %bitcast.6, f32[1]{0:T(128)} %bitcast.7), dimensions={0} | concatenate | bytes 56 | tf_op jit(solution)/shard_map/concatenate | solution.py:30
  152.4 17.2 %psum.15 = f32[7]{0:T(128)S(1)} all-reduce(f32[7]{0:T(128)S(1)} %concatenate.13), channel_id=1, replica_groups=mesh['section'=4,'tok'=8] {'tok'}, use_global_device_ids=true, to_apply=%region_9.10 | all-reduce | flops 7 | bytes 56 | tf_op jit(solution)/shard_map/psum | solution.py:70
  169.6 0.7 fusion.5
  170.2 3.2 %maximum_multiply_fusion = f32[3]{0:T(128)S(1)} fusion(f32[1]{0:T(128)} %get-tuple-element.18, f32[1]{0:T(128)} %get-tuple-element.19, f32[1]{0:T(128)} %get-tuple-element.20, f32[2]{0:T(128)S(1)} %bitcast.38, f32[1]{0:T(128)} %get-tuple-element.17, f32[1]{0:T(128)} %get-tuple-element.16), kind=kLoop, calls=%fused_computation.16 | loop fusion | flops 18 | bytes 40 | tf_op jit(solution)/shard_map/div | solution.py:39
  173.5 0.1 slice_bitcast_fusion.1
  173.6 0.7 copy.5
  174.2 0.0 copy-done
  (2 shorter events, 0.0 us)
Async XLA Ops:
  7.2 86.1 %all-gather.2.cloned.1.call-start = ((), (), s32[]{:S(2)}) async-start(), calls=%async_computation.1 | async-start | bytes 9437184 | tf_op jit(solution)/shard_map/all_gather | solution.py:51
  7.9 129.8 %reduce-scatter.2.cloned.1.call-start = ((), (), s32[]{:S(2)}) async-start(), calls=%async_computation.2 | async-start | bytes 2359296 | tf_op jit(solution)/shard_map/reduce_scatter | solution.py:61
  138.9 35.3 %copy-start = (f32[2,512,64]{1,2,0:T(8,128)}, f32[2,512,64]{1,2,0:T(8,128)S(1)}, u32[]{:S(2)}) copy-start(f32[2,512,64]{1,2,0:T(8,128)S(1)} %get-tuple-element.11) | copy-start | bytes 786436
  138.9 5.9 %collective-permute-start.1 = (bf16[512,64]{0,1:T(8,128)(2,1)S(1)}, bf16[512,64]{0,1:T(8,128)(2,1)S(1)}, u32[]{:S(2)}, u32[]{:S(2)}) collective-permute-start(bf16[512,64]{0,1:T(8,128)(2,1)S(1)} %get-tuple-element.13), channel_id=1, source_target_pairs={{8,0},{16,8},{24,16},{9,1},{17,9},{25,17},{10,2},{18,10},{26,18},{... | collective-permute-start | bytes 196616 | tf_op jit(solution)/shard_map/ppermute | solution.py:10
  142.0 6.4 %collective-permute-start = (bf16[512,64]{0,1:T(8,128)(2,1)S(1)}, bf16[512,64]{0,1:T(8,128)(2,1)S(1)}, u32[]{:S(2)}, u32[]{:S(2)}) collective-permute-start(bf16[512,64]{0,1:T(8,128)(2,1)S(1)} %get-tuple-element.12), channel_id=1, source_target_pairs={{0,8},{8,16},{16,24},{1,9},{9,17},{17,25},{2,10},{10,18},{18,26},{... | collective-permute-start | bytes 196616 | tf_op jit(solution)/shard_map/ppermute | solution.py:10
Sparse Core Ops, SparseCore 0:
  9.6 83.6 all-gather.1
  106.2 31.4 reduce-scatter.1
where the time goes:
time: 181 us
  waiting for transfers between devices  108 us (60%)
  blocking collectives  30.7 us (17%)
  between operations  14.1 us (8%)
  matrix products  12.8 us (7%)
  other arithmetic  5.78 us (3%)
  starting transfers between devices  5.36 us (3%)
  local copies, waits for them, and re-layouts  4.73 us (3%)
    all_gather x1, waiting for transfers between devices, local(): lax.all_gather(projection, 'tok', axis=0, tiled=True)  85.3 us
    reduce_scatter x1, waiting for transfers between devices, local(): shares = lax.psum_scatter(raw_gram, 'tok', scatter_dimension=2, tiled=True)  18.1 us
    psum x1, blocking collectives, local(): products = lax.psum(partial_products, 'tok')  17.2 us
    psum x1, blocking collectives, local(): totals = lax.psum(local_sums, 'tok')  13.5 us
    dot_general x1, matrix products, local(): jnp.dot(flat_acts, lax.all_gather(projection, 'tok', axis=0, tiled=True),...  9.49 us
    ppermute x2, starting transfers between devices, shifted(): return lax.ppermute(block, axis, route)  5.28 us
  transfers between devices with their start and end apart: 4, of which 3 were waited for; matrix products, arithmetic and copies ran while one was open for 0% of the time, Pallas kernels for 0%

commit v1 on v0

--- a/solution.py
+++ b/solution.py
@@ -67,7 +67,7 @@
         jnp.float32
     )
     partial_products = local_products(local_sketch, prev_last, next_first, section_index, sections)
-    products = lax.psum(partial_products, "tok")
+    products = jnp.sum(lax.all_gather(partial_products, "tok"), axis=0)
     return (local_sketch, finish(products, layers))
 
 

time: 181 us -> 182 us (level)
  waiting for transfers between devices: 108 us -> 106 us
    unnamed x0 -> x1, blocking collectives: none -> 17.2 us
    psum x1 -> x0, blocking collectives: 17.2 us -> none  [local(): products = lax.psum(partial_products, 'tok')]
  transfers between devices with their start and end apart: 4 -> 4, of which waited for: 3 -> 3; matrix products, arithmetic and copies ran while one was open for 0% -> 1% of each run, Pallas kernels for 0% -> 0%
where the time goes in v1:
time: 182 us
  waiting for transfers between devices  106 us (58%)
  blocking collectives  30.9 us (17%)
  between operations  14.8 us (8%)
  matrix products  12.8 us (7%)
  other arithmetic  5.81 us (3%)
  local copies, waits for them, and re-layouts  5.61 us (3%)
  starting transfers between devices  5.36 us (3%)
    all_gather x1, waiting for transfers between devices, local(): lax.all_gather(projection, 'tok', axis=0, tiled=True)  85.3 us
    unnamed x1, blocking collectives  17.2 us
    reduce_scatter x1, waiting for transfers between devices, local(): shares = lax.psum_scatter(raw_gram, 'tok', scatter_dimension=2, tiled=True)  16.7 us
    psum x1, blocking collectives, local(): totals = lax.psum(local_sums, 'tok')  13.6 us
    dot_general x1, matrix products, local(): jnp.dot(flat_acts, lax.all_gather(projection, 'tok', axis=0, tiled=True),...  9.49 us
    ppermute x2, starting transfers between devices, shifted(): return lax.ppermute(block, axis, route)  5.28 us
    ppermute x2, waiting for transfers between devices, shifted(): return lax.ppermute(block, axis, route)  3.76 us
  transfers between devices with their start and end apart: 4, of which 3 were waited for; matrix products, arithmetic and copies ran while one was open for 1% of the time, Pallas kernels for 0%

profile of v1, /device:TPU:5, one launch (start us, length us, event | category | flops | bytes accessed | tf_op | source)
XLA Modules:
  0.0 181.7 jit_solution(6030657810617556170)
XLA Ops:
  7.2 0.0 all-gather.3.cloned.1.call-start
  7.2 0.7 all-gather.3.cloned.1.call-update
  7.9 0.0 copy-start.1
  7.9 0.0 reduce-scatter.2.cloned.1.call-start
  8.0 85.3 %all-gather.3.cloned.1.call-done = bf16[8192,512]{1,0:T(8,128)(2,1)} async-done(((bf16[1024,512]{1,0:T(8,128)(2,1)}), bf16[8192,512]{1,0:T(8,128)(2,1)}) %all-gather.3.cloned.1.call-update) | async-done | bytes 8388624 | tf_op jit(solution)/shard_map/all_gather | solution.py:51
  93.2 9.5 %fusion.6 = (f32[2,512]{1,0:T(2,128)S(1)}, f32[2,256,512]{2,1,0:T(8,128)S(1)}) fusion(bf16[2,256,8192]{2,1,0:T(8,128)(2,1)} %param.2, bf16[8192,512]{1,0:T(8,128)(2,1)} %all-gather.3.cloned.1.call-done), kind=kOutput, calls=%fused_computation.23 | convolution fusion | flops 4295228416 | bytes 17829888 | tf_op jit(solution)/shard_map/dot_general | solution.py:49
  102.7 3.3 %fusion.7 = f32[2,512,512]{1,2,0:T(8,128)} fusion(f32[2,256,512]{2,1,0:T(8,128)S(1)} %get-tuple-element.22), kind=kOutput, calls=%fused_computation.24 | convolution fusion | flops 1610612736 | bytes 3145728 | tf_op jit(solution)/shard_map/ltr,lts->lrs/dot_general | solution.py:55
  106.0 0.0 reduce-scatter.2.cloned.1.call-update
  106.1 0.0 copy-done.1
  106.1 0.6 dynamic-slice
  107.3 13.6 %psum.7 = f32[2,512]{1,0:T(2,128)S(1)} all-reduce(f32[2,512]{1,0:T(2,128)S(1)} %get-tuple-element.21), channel_id=1, replica_groups=mesh['section'=4,'tok'=8] {'tok'}, use_global_device_ids=true, to_apply=%region_2.0 | all-reduce | flops 1024 | bytes 8192 | tf_op jit(solution)/shard_map/psum | solution.py:62
  121.0 0.1 constant_dynamic-slice_fusion
  121.0 16.7 %reduce-scatter.2.cloned.1.call-done = f32[2,512,64]{1,2,0:T(8,128)} async-done(((f32[2,512,512]{1,2,0:T(8,128)}), f32[2,512,64]{1,2,0:T(8,128)}) %reduce-scatter.2.cloned.1.call-update) | async-done | bytes 262160 | tf_op jit(solution)/shard_map/reduce_scatter | solution.py:61
  137.8 1.2 multiply_reduce_fusion
  138.9 0.0 copy-start
  139.0 3.1 %collective-permute-start.1 = (bf16[512,64]{0,1:T(8,128)(2,1)S(1)}, bf16[512,64]{0,1:T(8,128)(2,1)S(1)}, u32[]{:S(2)}, u32[]{:S(2)}) collective-permute-start(bf16[512,64]{0,1:T(8,128)(2,1)S(1)} %get-tuple-element.13), channel_id=1, source_target_pairs={{8,0},{16,8},{24,16},{9,1},{17,9},{25,17},{10,2},{18,10},{26,18},{... | collective-permute-start | bytes 196616 | tf_op jit(solution)/shard_map/ppermute | solution.py:10
  142.1 2.2 %collective-permute-start = (bf16[512,64]{0,1:T(8,128)(2,1)S(1)}, bf16[512,64]{0,1:T(8,128)(2,1)S(1)}, u32[]{:S(2)}, u32[]{:S(2)}) collective-permute-start(bf16[512,64]{0,1:T(8,128)(2,1)S(1)} %get-tuple-element.12), channel_id=1, source_target_pairs={{0,8},{8,16},{16,24},{1,9},{9,17},{17,25},{2,10},{10,18},{18,26},{... | collective-permute-start | bytes 196616 | tf_op jit(solution)/shard_map/ppermute | solution.py:10
  144.3 0.6 multiply_reduce_fusion.3
  144.9 0.0 collective-permute-done.1
  144.9 3.8 %collective-permute-done = bf16[512,64]{0,1:T(8,128)(2,1)S(1)} collective-permute-done((bf16[512,64]{0,1:T(8,128)(2,1)S(1)}, bf16[512,64]{0,1:T(8,128)(2,1)S(1)}, u32[]{:S(2)}, u32[]{:S(2)}) %collective-permute-start) | collective-permute-done | bytes 65568 | tf_op jit(solution)/shard_map/ppermute | solution.py:10
  148.7 0.7 multiply_reduce_fusion.1
  149.4 3.2 %concatenate.13 = f32[7]{0:T(128)S(1)} concatenate(f32[2]{0:T(128)S(1)} %get-tuple-element.10, f32[1]{0:T(128)} %bitcast.1, f32[1]{0:T(128)} %bitcast.4, f32[1]{0:T(128)} %bitcast.5, f32[1]{0:T(128)} %bitcast.6, f32[1]{0:T(128)} %bitcast.7), dimensions={0} | concatenate | bytes 56 | tf_op jit(solution)/shard_map/concatenate | solution.py:30
  152.6 0.2 dynamic-update-slice
  152.8 17.2 %all-reduce = f32[56]{0:T(128)S(1)} all-reduce(f32[56]{0:T(128)S(1)} %dynamic-update-slice), channel_id=2, replica_groups=mesh['section'=4,'tok'=8] {'tok'}, use_global_device_ids=true, to_apply=%add | all-reduce | flops 56 | bytes 448
  170.1 0.1 reshape.11
  170.2 0.7 fusion.5
  170.9 3.2 %maximum_multiply_fusion = f32[3]{0:T(128)S(1)} fusion(f32[1]{0:T(128)} %get-tuple-element.18, f32[1]{0:T(128)} %get-tuple-element.19, f32[1]{0:T(128)} %get-tuple-element.20, f32[2]{0:T(128)S(1)} %bitcast.39, f32[1]{0:T(128)} %get-tuple-element.17, f32[1]{0:T(128)} %get-tuple-element.16), kind=kLoop, calls=%fused_computation.16 | loop fusion | flops 18 | bytes 40 | tf_op jit(solution)/shard_map/div | solution.py:39
  174.1 0.1 slice_bitcast_fusion.1
  174.2 0.7 copy.5
  174.8 0.0 copy-done
  (4 shorter events, 0.1 us)
Async XLA Ops:
  7.2 86.1 %all-gather.3.cloned.1.call-start = ((), (), s32[]{:S(2)}) async-start(), calls=%async_computation.1 | async-start | bytes 9437184 | tf_op jit(solution)/shard_map/all_gather | solution.py:51
  7.9 98.2 %copy-start.1 = (u32[32]{0:T(128)S(1)}, u32[32]{0:T(128)}, u32[]{:S(2)}) copy-start(u32[32]{0:T(128)} %constant.24) | copy-start | bytes 388
  7.9 129.9 %reduce-scatter.2.cloned.1.call-start = ((), (), s32[]{:S(2)}) async-start(), calls=%async_computation.2 | async-start | bytes 2359296 | tf_op jit(solution)/shard_map/reduce_scatter | solution.py:61
  138.9 35.9 %copy-start = (f32[2,512,64]{1,2,0:T(8,128)}, f32[2,512,64]{1,2,0:T(8,128)S(1)}, u32[]{:S(2)}) copy-start(f32[2,512,64]{1,2,0:T(8,128)S(1)} %get-tuple-element.11) | copy-start | bytes 786436
  139.0 5.9 %collective-permute-start.1 = (bf16[512,64]{0,1:T(8,128)(2,1)S(1)}, bf16[512,64]{0,1:T(8,128)(2,1)S(1)}, u32[]{:S(2)}, u32[]{:S(2)}) collective-permute-start(bf16[512,64]{0,1:T(8,128)(2,1)S(1)} %get-tuple-element.13), channel_id=1, source_target_pairs={{8,0},{16,8},{24,16},{9,1},{17,9},{25,17},{10,2},{18,10},{26,18},{... | collective-permute-start | bytes 196616 | tf_op jit(solution)/shard_map/ppermute | solution.py:10
  142.1 6.6 %collective-permute-start = (bf16[512,64]{0,1:T(8,128)(2,1)S(1)}, bf16[512,64]{0,1:T(8,128)(2,1)S(1)}, u32[]{:S(2)}, u32[]{:S(2)}) collective-permute-start(bf16[512,64]{0,1:T(8,128)(2,1)S(1)} %get-tuple-element.12), channel_id=1, source_target_pairs={{0,8},{8,16},{16,24},{1,9},{9,17},{17,25},{2,10},{10,18},{18,26},{... | collective-permute-start | bytes 196616 | tf_op jit(solution)/shard_map/ppermute | solution.py:10
Sparse Core Ops, SparseCore 0:
  9.6 83.6 all-gather.2
  106.2 31.5 reduce-scatter.1

commit v2 on v0

--- a/solution.py
+++ b/solution.py
@@ -48,7 +48,9 @@
     flat_acts = activations.reshape(layers * tok_rows, model_width)
     projected = jnp.dot(
         flat_acts,
-        lax.all_gather(projection, "tok", axis=0, tiled=True),
+        jnp.concatenate(
+            lax.all_to_all(jnp.stack([projection] * lax.axis_size("tok")), "tok", 0, 0), axis=0
+        ),
         preferred_element_type=jnp.float32,
     )
     projected = projected.reshape(layers, tok_rows, sketch_width)

time: 181 us -> 285 us (1.57)
  blocking collectives: 30.7 us -> 220 us
  waiting for transfers between devices: 108 us -> 22.1 us
    all_to_all x0 -> x1, blocking collectives: none -> 188 us  [local(): lax.all_to_all(jnp.stack([projection] * lax.axis_size('tok')), 'tok', 0, 0)]
    all_gather x1 -> x0, waiting for transfers between devices: 85.3 us -> none  [local(): lax.all_gather(projection, 'tok', axis=0, tiled=True)]
  transfers between devices with their start and end apart: 4 -> 3, of which waited for: 3 -> 2; matrix products, arithmetic and copies ran while one was open for 0% -> 0% of each run, Pallas kernels for 0% -> 0%
where the time goes in v2:
time: 285 us; the launch traced here: 284 us
  blocking collectives  220 us (77%)
  waiting for transfers between devices  22.1 us (8%)
  between operations  14.1 us (5%)
  matrix products  10.4 us (4%)
  local copies, waits for them, and re-layouts  6.69 us (2%)
  other arithmetic  5.78 us (2%)
  starting transfers between devices  5.32 us (2%)
    all_to_all x1, blocking collectives, local(): lax.all_to_all(jnp.stack([projection] * lax.axis_size('tok')), 'tok', 0, 0)  188 us
    reduce_scatter x1, waiting for transfers between devices, local(): shares = lax.psum_scatter(raw_gram, 'tok', scatter_dimension=2, tiled=True)  18.3 us
    psum x1, blocking collectives, local(): products = lax.psum(partial_products, 'tok')  17.4 us
    psum x1, blocking collectives, local(): totals = lax.psum(local_sums, 'tok')  14.3 us
    dot_general x1, matrix products, local(): jnp.dot(flat_acts, jnp.concatenate(lax.all_to_all(jnp.stack([projection]...  7.11 us
  transfers between devices with their start and end apart: 3, of which 2 were waited for; matrix products, arithmetic and copies ran while one was open for 0% of the time, Pallas kernels for 0%

profile of v2, /device:TPU:5, one launch (start us, length us, event | category | flops | bytes accessed | tf_op | source)
XLA Modules:
  0.0 284.3 jit_solution(14092672945231971822)
XLA Ops:
  7.2 0.0 reduce-scatter.2.cloned.1.call-start
  7.2 2.0 stack.32
  9.2 188.2 %all_to_all.5 = bf16[8,1024,512]{2,1,0:T(8,128)(2,1)S(1)} all-to-all(bf16[8,1024,512]{2,1,0:T(8,128)(2,1)S(1)} %stack.32), channel_id=1, replica_groups=mesh['section'=4,'tok'=8] {'tok'}, dimensions={0} | all-to-all | bytes 16777216 | tf_op jit(solution)/shard_map/all_to_all | solution.py:52
  197.3 7.1 %fusion.4 = (f32[2,512]{1,0:T(2,128)S(1)}, f32[2,256,512]{2,1,0:T(8,128)S(1)}) fusion(bf16[2,256,8192]{2,1,0:T(8,128)(2,1)} %param.2, bf16[8192,512,1]{1,0,2:T(8,128)(2,1)S(1)} %bitcast.37), kind=kOutput, calls=%fused_computation.21 | convolution fusion | flops 4295228416 | bytes 17829888 | tf_op jit(solution)/shard_map/dot_general | solution.py:49
  204.5 3.3 %fusion.5 = f32[2,512,512]{1,2,0:T(8,128)} fusion(f32[2,256,512]{2,1,0:T(8,128)S(1)} %get-tuple-element.22), kind=kOutput, calls=%fused_computation.22 | convolution fusion | flops 1610612736 | bytes 3145728 | tf_op jit(solution)/shard_map/ltr,lts->lrs/dot_general | solution.py:57
  207.8 0.0 reduce-scatter.2.cloned.1.call-update
  207.8 14.3 %psum.14 = f32[2,512]{1,0:T(2,128)S(1)} all-reduce(f32[2,512]{1,0:T(2,128)S(1)} %get-tuple-element.21), channel_id=1, replica_groups=mesh['section'=4,'tok'=8] {'tok'}, use_global_device_ids=true, to_apply=%region_2.0 | all-reduce | flops 1024 | bytes 8192 | tf_op jit(solution)/shard_map/psum | solution.py:64
  222.1 0.1 constant_dynamic-slice_fusion
  222.2 18.3 %reduce-scatter.2.cloned.1.call-done = f32[2,512,64]{1,2,0:T(8,128)} async-done(((f32[2,512,512]{1,2,0:T(8,128)}), f32[2,512,64]{1,2,0:T(8,128)}) %reduce-scatter.2.cloned.1.call-update) | async-done | bytes 262160 | tf_op jit(solution)/shard_map/reduce_scatter | solution.py:63
  240.5 1.2 multiply_reduce_fusion
  241.7 0.0 copy-start
  241.7 3.1 %collective-permute-start.1 = (bf16[512,64]{0,1:T(8,128)(2,1)S(1)}, bf16[512,64]{0,1:T(8,128)(2,1)S(1)}, u32[]{:S(2)}, u32[]{:S(2)}) collective-permute-start(bf16[512,64]{0,1:T(8,128)(2,1)S(1)} %get-tuple-element.13), channel_id=1, source_target_pairs={{8,0},{16,8},{24,16},{9,1},{17,9},{25,17},{10,2},{18,10},{26,18},{... | collective-permute-start | bytes 196616 | tf_op jit(solution)/shard_map/ppermute | solution.py:10
  244.8 2.2 collective-permute-start
  247.0 0.6 multiply_reduce_fusion.3
  247.6 0.0 collective-permute-done.1
  247.6 3.7 %collective-permute-done = bf16[512,64]{0,1:T(8,128)(2,1)S(1)} collective-permute-done((bf16[512,64]{0,1:T(8,128)(2,1)S(1)}, bf16[512,64]{0,1:T(8,128)(2,1)S(1)}, u32[]{:S(2)}, u32[]{:S(2)}) %collective-permute-start) | collective-permute-done | bytes 65568 | tf_op jit(solution)/shard_map/ppermute | solution.py:10
  251.3 0.7 multiply_reduce_fusion.1
  252.1 3.2 %concatenate.13 = f32[7]{0:T(128)S(1)} concatenate(f32[2]{0:T(128)S(1)} %get-tuple-element.10, f32[1]{0:T(128)} %bitcast.2, f32[1]{0:T(128)} %bitcast.5, f32[1]{0:T(128)} %bitcast.6, f32[1]{0:T(128)} %bitcast.7, f32[1]{0:T(128)} %bitcast.8), dimensions={0} | concatenate | bytes 56 | tf_op jit(solution)/shard_map/concatenate | solution.py:30
  255.3 17.4 %psum.15 = f32[7]{0:T(128)S(1)} all-reduce(f32[7]{0:T(128)S(1)} %concatenate.13), channel_id=1, replica_groups=mesh['section'=4,'tok'=8] {'tok'}, use_global_device_ids=true, to_apply=%region_9.10 | all-reduce | flops 7 | bytes 56 | tf_op jit(solution)/shard_map/psum | solution.py:72
  272.8 0.7 fusion.3
  273.4 3.2 %maximum_multiply_fusion = f32[3]{0:T(128)S(1)} fusion(f32[1]{0:T(128)} %get-tuple-element.18, f32[1]{0:T(128)} %get-tuple-element.19, f32[1]{0:T(128)} %get-tuple-element.20, f32[2]{0:T(128)S(1)} %bitcast.38, f32[1]{0:T(128)} %get-tuple-element.17, f32[1]{0:T(128)} %get-tuple-element.16), kind=kLoop, calls=%fused_computation.14 | loop fusion | flops 18 | bytes 40 | tf_op jit(solution)/shard_map/div | solution.py:39
  276.7 0.1 slice_bitcast_fusion.1
  276.7 0.7 copy.5
  277.4 0.0 copy-done
  (2 shorter events, 0.0 us)
Async XLA Ops:
  7.2 233.3 %reduce-scatter.2.cloned.1.call-start = ((), (), s32[]{:S(2)}) async-start(), calls=%async_computation.2 | async-start | bytes 2359296 | tf_op jit(solution)/shard_map/reduce_scatter | solution.py:63
  241.7 35.8 %copy-start = (f32[2,512,64]{1,2,0:T(8,128)}, f32[2,512,64]{1,2,0:T(8,128)S(1)}, u32[]{:S(2)}) copy-start(f32[2,512,64]{1,2,0:T(8,128)S(1)} %get-tuple-element.11) | copy-start | bytes 786436
  241.7 5.9 %collective-permute-start.1 = (bf16[512,64]{0,1:T(8,128)(2,1)S(1)}, bf16[512,64]{0,1:T(8,128)(2,1)S(1)}, u32[]{:S(2)}, u32[]{:S(2)}) collective-permute-start(bf16[512,64]{0,1:T(8,128)(2,1)S(1)} %get-tuple-element.13), channel_id=1, source_target_pairs={{8,0},{16,8},{24,16},{9,1},{17,9},{25,17},{10,2},{18,10},{26,18},{... | collective-permute-start | bytes 196616 | tf_op jit(solution)/shard_map/ppermute | solution.py:10
  244.8 6.5 %collective-permute-start = (bf16[512,64]{0,1:T(8,128)(2,1)S(1)}, bf16[512,64]{0,1:T(8,128)(2,1)S(1)}, u32[]{:S(2)}, u32[]{:S(2)}) collective-permute-start(bf16[512,64]{0,1:T(8,128)(2,1)S(1)} %get-tuple-element.12), channel_id=1, source_target_pairs={{0,8},{8,16},{16,24},{1,9},{9,17},{17,25},{2,10},{10,18},{18,26},{... | collective-permute-start | bytes 196616 | tf_op jit(solution)/shard_map/ppermute | solution.py:10
Sparse Core Ops, SparseCore 0:
  207.9 32.5 reduce-scatter.1
